TPU v7x, 256 devices: a whole 4x4x8 slice. The times are simulated.
256 devices in a mesh: rows: 128 (over x, z, y), cols: 2 (over core).
Axes of the slice: x: 4, y: 4, z: 8, core: 2. Of those that a mesh axis runs over, the one named last changes fastest.
Arguments:
- points: float32 [8, 32768], P(None, ('cols', 'rows')), may hold values from -6 to 6
- targets: float32 [32768], P(('cols', 'rows')), may hold values from -6 to 6
- noise: float32 [64, 32768], P(None, ('cols', 'rows')), may hold values from -6 to 6
- omega: float32 [8, 2048], P(None, 'rows'), may hold values from -12 to 12
- phase: float32 [2048], P('rows'), may hold values from -3.140625 to 3.140625
- weights: float32 [2048, 64], P('rows'), may hold values from -6 to 6
Outputs:
- posterior: float32 [64, 32768], P(None, ('cols', 'rows'))
- residual: float32 [64, 32768], P(None, ('cols', 'rows'))
All inputs are finite; a program needn't handle non-finite values.
Results may differ from a plain program's by a relative error of at most 0.02.
Values may be sent and summed in bfloat16 or wider, within the bound.
A program may use at most 64 MiB of HBM per device.

v0:
```python
import functools
import math

import jax
import jax.numpy as jnp
from jax import lax
from jax.sharding import Mesh
from jax.sharding import PartitionSpec as P

ITERS = 2
ROWS = ("rows_0", "rows_1", "rows_2")
ROWS_COLS = ("rows_0", "rows_1", "rows_2", "cols")
COLS_ROWS = ("cols", "rows_0", "rows_1", "rows_2")


def turned_gather(arrays, axis, dims):
    turned = [jnp.moveaxis(a, dim, 0) for a, dim in zip(arrays, dims)]
    both = jnp.concatenate([t.reshape(len(t), -1) for t in turned], axis=1)
    whole, at, finished = (lax.all_gather(both, axis, axis=0, tiled=True), 0, [])
    for t, dim in zip(turned, dims):
        section = whole[:, at : at + t[0].size].reshape(-1, *t.shape[1:])
        finished.append(jnp.moveaxis(section, 0, dim))
        at += t[0].size
    return tuple(finished)


def over_axes(value, axes):
    return functools.reduce(lax.psum, axes, value)


def kernel_block(left, right):
    cross = lax.dot_general(
        left,
        right,
        (((0,), (0,)), ((), ())),
        precision=lax.Precision.HIGHEST,
        preferred_element_type=jnp.float32,
    )
    left_sq = jnp.sum(left * left, 0)
    right_sq = jnp.sum(right * right, 0)
    dist = left_sq[:, None] + right_sq[None, :] - 2.0 * cross
    return jnp.exp(-2.0 * dist).astype(jnp.bfloat16)


def body(points, targets, noise, omega, phase, weights):
    wide_omega, wide_phase, wide_weights = turned_gather((omega, phase, weights), ROWS, (1, 0, 0))
    features = jnp.cos(
        lax.dot_general(
            wide_omega,
            points,
            (((0,), (0,)), ((), ())),
            precision=lax.Precision.HIGHEST,
            preferred_element_type=jnp.float32,
        )
        + wide_phase[:, None]
    )
    prior = math.sqrt(2.0 / wide_weights.shape[0]) * lax.dot_general(
        wide_weights,
        features,
        (((0,), (0,)), ((), ())),
        precision=lax.Precision.HIGHEST,
        preferred_element_type=jnp.float32,
    )
    rhs = targets[None, :] - prior - 0.5 * noise
    columns = lax.all_gather(points, ROWS_COLS, axis=1, tiled=True)
    residual = rhs
    direction = rhs
    posterior = prior
    norm_now = over_axes(jnp.sum(residual * residual, 1), ROWS_COLS)
    for step in range(ITERS):
        low = direction.astype(jnp.bfloat16)
        kernel_part = jnp.dot(
            lax.all_gather(low, ROWS_COLS, axis=1, tiled=True),
            kernel_block(columns, points),
            preferred_element_type=jnp.float32,
        )
        image = kernel_part + 0.25 * direction
        curve, mixed, square = (
            over_axes(jnp.sum(direction * image, 1), ROWS_COLS),
            over_axes(jnp.sum(residual * image, 1), ROWS_COLS),
            over_axes(jnp.sum(image * image, 1), ROWS_COLS),
        )
        alpha = norm_now / curve
        norm_next = norm_now - 2.0 * alpha * mixed + alpha * alpha * square
        posterior = posterior + alpha[:, None] * kernel_part
        residual = residual - alpha[:, None] * image
        if step + 1 < ITERS:
            direction = residual + (norm_next / norm_now)[:, None] * direction
            norm_now = norm_next
    return (posterior, residual)


def solution(mesh):
    finer = Mesh(
        mesh.devices.reshape(4, 8, 4, mesh.shape["cols"]), ("rows_0", "rows_1", "rows_2", "cols")
    )
    in_specs = (
        P(None, COLS_ROWS),
        P(COLS_ROWS),
        P(None, COLS_ROWS),
        P(None, ROWS),
        P(ROWS),
        P(ROWS, None),
    )
    out_specs = (P(None, COLS_ROWS), P(None, COLS_ROWS))
    return jax.shard_map(body, mesh=finer, in_specs=in_specs, out_specs=out_specs, check_vma=False)
```

profile of v0, /device:TPU:1, one launch (start us, length us, event | category | flops | bytes accessed | tf_op | source)
XLA Modules:
  0.0 662.3 jit_solution(5400117945138848023)
XLA Ops:
  7.2 0.0 all-gather.6.cloned.1.call-start
  7.2 0.7 all-gather.6.cloned.1.call-update
  7.9 0.0 all-gather.4.cloned.1.call-start
  7.9 0.8 copy.10
  8.7 0.7 copy.11
  9.4 0.8 pad_maximum_fusion
  10.2 300.3 %all_gather.12 = f32[2048,73]{1,0:T(8,128)S(1)} all-gather(f32[16,73]{1,0:T(8,128)S(1)} %pad_maximum_fusion), channel_id=1, replica_groups=mesh['rows_0'=4,'rows_1'=8,'rows_2'=4,'cols'=2] {'rows_0','rows_1','rows..., dimensions={0}, use_global_device_ids=true | all-gather | bytes 602688 | tf_op jit(solution)/shard_map/all_gather | solution.py:19
  310.6 0.6 slice_reduce_fusion
  311.2 6.0 fusion.4
  317.2 3.6 fusion.9
  320.8 0.0 all-gather.4.cloned.1.call-update
  320.8 0.2 all-gather.8.cloned.1.call-start
  321.1 0.7 multiply_reduce_fusion.5
  321.8 0.0 all-gather.6.cloned.1.call-done
  321.8 1.5 multiply_reduce_fusion
  323.3 33.1 %fusion.3 = bf16[32768,128]{1,0:T(8,128)(2,1)} fusion(f32[8,32768]{1,0:T(8,128)} %all-gather.6.cloned.1.call-done, f32[8,128]{1,0:T(8,128)} %param.6, f32[128]{0:T(128)S(1)} %multiply_reduce_fusion.5, f32[32768]{0:T(1024)S(1)} %multiply_reduce_fusion), kind=kOutput, calls=%fused_computation.4 | convolution fusion | flops 423624704 | bytes 9572864 | tf_op jit(solution)/shard_map/dot_general | solution.py:32
  356.4 110.6 %all-gather.4.cloned.1.call-done = bf16[64,32768]{1,0:T(8,128)(2,1)} async-done(((bf16[64,128]{1,0:T(8,128)(2,1)}), bf16[64,32768]{1,0:T(8,128)(2,1)}) %all-gather.4.cloned.1.call-update) | async-done | bytes 4194320 | tf_op jit(solution)/shard_map/all_gather | solution.py:73
  467.0 6.4 multiply_reduce_fusion.3
  473.3 8.3 %all-reduce.2 = (f32[64]{0:T(128)S(1)}, f32[64]{0:T(128)S(1)}, f32[64]{0:T(128)S(1)}) all-reduce(f32[64]{0:T(128)S(1)} %get-tuple-element.3, f32[64]{0:T(128)S(1)} %get-tuple-element.4, f32[64]{0:T(128)S(1)} %get-tuple-element.2), channel_id=1, replica_groups=mesh['rows_0'=4,'rows_1'=8,'rows_2'=4,'cols'=2] {'rows_0'}, use_global_device_ids=true, to_apply=%region_13.0 | all-reduce | flops 192 | bytes 1536 | tf_op jit(solution)/shard_map/psum | solution.py:28
  481.7 13.1 %all-reduce = (f32[64]{0:T(128)S(1)}, f32[64]{0:T(128)S(1)}, f32[64]{0:T(128)S(1)}) all-reduce(f32[64]{0:T(128)S(1)} %get-tuple-element.11, f32[64]{0:T(128)S(1)} %get-tuple-element.12, f32[64]{0:T(128)S(1)} %get-tuple-element.13), channel_id=1, replica_groups=mesh['rows_0'=4,'rows_1'=8,'rows_2'=4,'cols'=2] {'rows_1'}, use_global_device_ids=true, to_apply=%region_14.0 | all-reduce | flops 192 | bytes 1536 | tf_op jit(solution)/shard_map/psum | solution.py:28
  494.8 8.4 %all-reduce.1 = (f32[64]{0:T(128)S(1)}, f32[64]{0:T(128)S(1)}, f32[64]{0:T(128)S(1)}) all-reduce(f32[64]{0:T(128)S(1)} %get-tuple-element.5, f32[64]{0:T(128)S(1)} %get-tuple-element.6, f32[64]{0:T(128)S(1)} %get-tuple-element.7), channel_id=1, replica_groups=mesh['rows_0'=4,'rows_1'=8,'rows_2'=4,'cols'=2] {'rows_2'}, use_global_device_ids=true, to_apply=%region_15.0 | all-reduce | flops 192 | bytes 1536 | tf_op jit(solution)/shard_map/psum | solution.py:28
  503.2 10.2 %all-reduce.3 = (f32[64]{0:T(128)S(1)}, f32[64]{0:T(128)S(1)}, f32[64]{0:T(128)S(1)}) all-reduce(f32[64]{0:T(128)S(1)} %get-tuple-element.8, f32[64]{0:T(128)S(1)} %get-tuple-element.9, f32[64]{0:T(128)S(1)} %get-tuple-element.10), channel_id=1, replica_groups=mesh['rows_0'=4,'rows_1'=8,'rows_2'=4,'cols'=2] {'cols'}, use_global_device_ids=true, to_apply=%region_16.0 | all-reduce | flops 192 | bytes 1536 | tf_op jit(solution)/shard_map/psum | solution.py:28
  513.4 0.7 fusion.7
  514.1 0.0 all-gather.8.cloned.1.call-update
  514.1 94.5 %all-gather.8.cloned.1.call-done = bf16[64,32768]{1,0:T(8,128)(2,1)} async-done(((bf16[64,128]{1,0:T(8,128)(2,1)}), bf16[64,32768]{1,0:T(8,128)(2,1)}) %all-gather.8.cloned.1.call-update) | async-done | bytes 4194320 | tf_op jit(solution)/shard_map/all_gather | solution.py:73
  608.7 6.3 multiply_reduce_fusion.1
  615.0 8.3 %psum.136 = f32[64]{0:T(128)S(1)} all-reduce(f32[64]{0:T(128)S(1)} %get-tuple-element.26), channel_id=1, replica_groups=mesh['rows_0'=4,'rows_1'=8,'rows_2'=4,'cols'=2] {'rows_0'}, use_global_device_ids=true, to_apply=%region_18.0 | all-reduce | flops 64 | bytes 512 | tf_op jit(solution)/shard_map/psum | solution.py:28
  623.4 13.1 %psum.137 = f32[64]{0:T(128)S(1)} all-reduce(f32[64]{0:T(128)S(1)} %psum.136), channel_id=1, replica_groups=mesh['rows_0'=4,'rows_1'=8,'rows_2'=4,'cols'=2] {'rows_1'}, use_global_device_ids=true, to_apply=%region_19.0 | all-reduce | flops 64 | bytes 512 | tf_op jit(solution)/shard_map/psum | solution.py:28
  636.5 8.4 %psum.138 = f32[64]{0:T(128)S(1)} all-reduce(f32[64]{0:T(128)S(1)} %psum.137), channel_id=1, replica_groups=mesh['rows_0'=4,'rows_1'=8,'rows_2'=4,'cols'=2] {'rows_2'}, use_global_device_ids=true, to_apply=%region_20.0 | all-reduce | flops 64 | bytes 512 | tf_op jit(solution)/shard_map/psum | solution.py:28
  644.9 10.2 %psum.139 = f32[64]{0:T(128)S(1)} all-reduce(f32[64]{0:T(128)S(1)} %psum.138), channel_id=1, replica_groups=mesh['rows_0'=4,'rows_1'=8,'rows_2'=4,'cols'=2] {'cols'}, use_global_device_ids=true, to_apply=%region_21.0 | all-reduce | flops 64 | bytes 512 | tf_op jit(solution)/shard_map/psum | solution.py:28
  655.1 0.7 multiply_subtract_fusion
  (2 shorter events, 0.0 us)
Async XLA Ops:
  7.2 314.6 %all-gather.6.cloned.1.call-start = ((), (), s32[]{:S(2)}) async-start(), calls=%async_computation.1 | async-start | bytes 1052672 | tf_op jit(solution)/shard_map/all_gather | solution.py:65
  7.9 459.1 %all-gather.4.cloned.1.call-start = ((), (), s32[]{:S(2)}) async-start(), calls=%async_computation | async-start | bytes 4210688 | tf_op jit(solution)/shard_map/all_gather | solution.py:73
  320.8 287.8 %all-gather.8.cloned.1.call-start = ((), (), s32[]{:S(2)}) async-start(), calls=%async_computation.2 | async-start | bytes 4210688 | tf_op jit(solution)/shard_map/all_gather | solution.py:73
Sparse Core Ops, SparseCore 0:
  11.7 107.1 all-gather.5
  321.0 145.9 all-gather.3
  514.2 94.3 all-gather.7
where the time goes:
time: 663 us; the launch traced here: 662 us
  blocking collectives  380 us (57%)
  waiting for transfers between devices  206 us (31%)
  matrix products  55.4 us (8%)
  between operations  13.8 us (2%)
    all_gather x1, blocking collectives, turned_gather(): lax.all_gather(both, axis, axis=0, tiled=True)  300 us
    all_gather x2, waiting for transfers between devices, body(): lax.all_gather(low, ROWS_COLS, axis=1, tiled=True)  205 us
    psum x8, blocking collectives, over_axes(): return functools.reduce(lax.psum, axes, value)  80.1 us
    dot_general x1, matrix products, kernel_block(): lax.dot_general(left, right, (((0,), (0,)), ((), ())), precision=lax.Prec...  33.1 us
  transfers between devices with their start and end apart: 3, of which 2 were waited for; matrix products, arithmetic and copies ran while one was open for 7% of the time, Pallas kernels for 0%

commit v1 on v0

v1 whole, which is shorter than its diff:
```python
import functools
import math

import jax
import jax.numpy as jnp
from jax import lax
from jax.experimental import pallas as pl
from jax.experimental.pallas import tpu as pltpu
from jax.sharding import Mesh
from jax.sharding import PartitionSpec as P

AXES = ("px", "pz", "py", "cols")
ROWS = ("px", "pz", "py")
COLS_ROWS = ("cols", "px", "pz", "py")
MESH = pl.DeviceIdType.MESH
F32, BF16 = jnp.float32, jnp.bfloat16

D = 8
S = 64
B = 128
FB = 16
JITTER = 0.25
SPREAD = math.sqrt(4.0 * math.log2(math.e))
SINE = [(-1) ** k * (2.0 * math.pi) ** (2 * k + 1) / math.factorial(2 * k + 1) for k in range(6)]


def SLOTS(nz, np_):
    table = [("prm_z", nz), ("prm_p", np_), ("pts_z", nz), ("pts_p", np_), ("pts_d", np_), ("prior", 1)]
    for n in "01":
        table += [("low%s_p" % n, np_), ("low%s_d" % n, np_), ("low%s_z" % n, nz), ("out%s" % n, nz)]
    for name in ("cur0", "cur1", "mom"):
        table += [(name + "_z", 2 * nz), (name + "_p", np_)]
    return table


def three_parts(a):
    one = a.astype(BF16).astype(F32)
    rest = a - one
    two = rest.astype(BF16).astype(F32)
    three = (rest - two).astype(BF16).astype(F32)
    return one, two, three


def rows_of(pieces, width):
    row = lax.broadcasted_iota(jnp.int32, (8, width), 0)
    out = jnp.zeros((8, width), F32)
    for k, piece in enumerate(pieces):
        out = jnp.where(row == k, piece, out)
    return out


def exponent_left(points):
    scaled = points * SPREAD
    a1, a2, a3 = three_parts(scaled)
    n1, n2, n3 = three_parts(-0.5 * jnp.sum(scaled * scaled, 0, keepdims=True))
    width = points.shape[1]
    norms = rows_of((n1, n2, n3, 1.0, 1.0, 1.0), width)
    return jnp.concatenate([a1, a1, a2, a2, a1, a3, norms, jnp.zeros((8, width), F32)], 0)


def exponent_right(points):
    scaled = points * SPREAD
    b1, b2, b3 = three_parts(scaled)
    n1, n2, n3 = three_parts(-0.5 * jnp.sum(scaled * scaled, 0, keepdims=True))
    width = points.shape[1]
    norms = rows_of((1.0, 1.0, 1.0, n1, n2, n3), width)
    return jnp.concatenate([b1, b2, b1, b2, b3, b1, norms, jnp.zeros((8, width), F32)], 0)


def cos_turns(t):
    r = t - jnp.floor(t + 0.5)
    v = 0.25 - jnp.abs(r)
    w = v * v
    acc = jnp.full_like(w, SINE[-1])
    for c in SINE[-2::-1]:
        acc = acc * w + c
    return acc * v


def mm(a, b, dims=(((1,), (0,)), ((), ()))):
    return lax.dot_general(a, b, dims, preferred_element_type=F32)


def kernel(
    sizes,
    pts_ref, tgt_ref, noise_ref, prm_ref,
    post_ref, res_ref,
    prm, ptsj, ptsi, pside, prior_s, acc, rhs_s, low, low_z, right, kern, outb, rcv,
    mom_z, mom_p, cur_z, cur_p, send, recv,
):
    nx, nz, ny = sizes
    np_, half = nx * ny, nz // 2
    nfeat = nx * nz * ny * FB
    x, z, y, c = (lax.axis_index(a) for a in AXES)
    p = x * ny + y
    oc = 1 - c
    twin = (x, z, y, oc)

    at = {}
    top = 0
    for name, count in SLOTS(nz, np_):
        at[name] = top
        top += count

    def rdma(name, k, src, dst, dev):
        i = at[name] + k
        return pltpu.make_async_remote_copy(
            src_ref=src, dst_ref=dst, send_sem=send.at[i], recv_sem=recv.at[i],
            device_id=dev, device_id_type=MESH)

    def plane(d, sign=1):
        dx, dy = lax.div(d, ny), lax.rem(d, ny)
        if sign < 0:
            dx, dy = nx - dx, ny - dy
        return lax.rem(x + dx, nx), lax.rem(y + dy, ny)

    def plane_dev(d):
        xx, yy = plane(d)
        return (xx, z, yy, c)

    def plane_slot(d):
        xx, yy = plane(d, -1)
        return xx * ny + yy

    def zdev(d, core):
        return (x, lax.rem(z + d, nz), y, core)

    def zfrom(d):
        return lax.rem(z + nz - d, nz)

    def loop(lo, hi, f):
        def step(i, carry):
            f(i)
            return carry
        lax.fori_loop(lo, hi, step, 0)

    bar = pltpu.get_barrier_semaphore()

    def greet(dev):
        pl.semaphore_signal(bar, inc=1, device_id=dev, device_id_type=MESH)

    greet(twin)
    loop(1, nz, lambda d: greet(zdev(d, c)))
    loop(1, nz, lambda d: greet(zdev(d, oc)))
    loop(1, np_, lambda d: greet(plane_dev(d)))
    pl.semaphore_wait(bar, 1 + 2 * (nz - 1) + np_ - 1)

    mine = lax.rem(z, 2) == c
    zslot = lax.div(z, 2)

    @pl.when(mine)
    def _():
        loop(1, nz, lambda d: rdma("prm_z", d, prm_ref, prm.at[p, zslot], zdev(d, c)).start())
        prm[p, zslot] = prm_ref[...]

    rdma("pts_d", 0, pts_ref, ptsj.at[c * np_ + p], twin).start()
    loop(1, np_, lambda d: rdma("pts_p", d, pts_ref, ptsj.at[c * np_ + p], plane_dev(d)).start())
    loop(1, nz, lambda d: rdma("pts_z", d, pts_ref, ptsi.at[z], zdev(d, c)).start())
    ptsj[c * np_ + p] = pts_ref[...]
    ptsi[z] = pts_ref[...]

    def got(name, k, dst):
        rdma(name, k, dst, dst, twin).wait_recv()

    def prm_wait(k):
        d = 2 * k
        src = zfrom(d)
        got("prm_z", d, prm.at[p, lax.div(src, 2)])

    def prm_wait_odd(k):
        d = 2 * k + 1
        src = zfrom(d)
        got("prm_z", d, prm.at[p, lax.div(src, 2)])

    @pl.when(mine)
    def _():
        loop(1, half, prm_wait)

    @pl.when(jnp.logical_not(mine))
    def _():
        loop(0, half, prm_wait_odd)

    loop(1, np_, lambda d: rdma("prm_p", d, prm.at[p], prm.at[p], plane_dev(d)).start())

    def pts_forward(d):
        slot = ptsj.at[c * np_ + plane_slot(d)]
        got("pts_p", d, slot)
        rdma("pts_d", d, slot, slot, twin).start()

    loop(1, np_, pts_forward)
    loop(1, nz, lambda d: got("pts_z", d, ptsi.at[zfrom(d)]))
    got("pts_d", 0, ptsj.at[oc * np_ + p])
    loop(1, np_, lambda d: got("pts_d", d, ptsj.at[oc * np_ + plane_slot(d)]))

    for t in range(half):
        two = jnp.concatenate([ptsi[2 * t], ptsi[2 * t + 1]], 1)
        right[t] = exponent_right(two).astype(BF16)

    def kern_block(j):
        two = jnp.concatenate([ptsj[2 * j], ptsj[2 * j + 1]], 1)
        left = exponent_left(two).T.astype(BF16)
        row = pl.multiple_of(j * 2 * B, 2 * B)
        for t in range(half):
            kern[t, pl.ds(row, 2 * B), :] = jnp.exp2(mm(left, right[t])).astype(BF16)

    loop(0, np_, kern_block)

    both = jnp.concatenate([pts_ref[...], ptsj[oc * np_ + p]], 1)
    b1, b2, b3 = three_parts(both)
    none = jnp.zeros((64, 2 * B), F32)
    ones = rows_of((1.0, 1.0, 1.0), 2 * B)
    tail = none[:32]
    pside[0] = jnp.concatenate([none, b1, b1, b1, ones, tail], 0).astype(BF16)
    pside[1] = jnp.concatenate([none, b2, b2, none[:16], tail, none[:0]][:5], 0).astype(BF16)
    pside[2] = jnp.concatenate([none, b3, none[:24], tail], 0).astype(BF16)
    prior_s[...] = jnp.zeros_like(prior_s)

    def prior_chunk(i):
        def one_wait(dy):
            d = i * ny + dy
            got("prm_p", d, prm.at[plane_slot(d)])

        @pl.when(i == 0)
        def _():
            loop(1, ny, one_wait)

        @pl.when(i > 0)
        def _():
            loop(0, ny, one_wait)

        xx = lax.rem(x + nx - i, nx)
        part = prm[pl.ds(xx * ny, ny)].reshape(ny * half * FB, 128)
        turns = mm(part, pside[0]) + mm(part, pside[1]) + mm(part, pside[2])
        feats = cos_turns(turns)
        f1 = feats.astype(BF16)
        f2 = (feats - f1.astype(F32)).astype(BF16)
        flip = (((0,), (0,)), ((), ()))
        prior_s[...] += (mm(part, f1, flip) + mm(part, f2, flip))[:S]

    loop(0, nx, prior_chunk)

    outb[0, 0] = prior_s[:, B:]
    rdma("prior", 0, outb.at[0, 0], rcv.at[2, 0], twin).start()
    got("prior", 0, rcv.at[2, 0])
    scale = math.sqrt(2.0 / nfeat)
    prior = scale * (prior_s[:, :B] + rcv[2, 0])
    rhs = tgt_ref[...] - prior - 0.5 * noise_ref[...]
    rhs_s[0] = prior
    rhs_s[1] = rhs
    rdma("prior", 0, outb.at[0, 0], rcv.at[2, 0], twin).wait_send()

    def matvec(n, field, first, each, last):
        pn, dn, zn, on = "low%d_p" % n, "low%d_d" % n, "low%d_z" % n, "out%d" % n
        own = low.at[n, c * np_ + p]
        low[n, c * np_ + p] = field.astype(BF16)
        loop(1, np_, lambda d: rdma(pn, d, own, own, plane_dev(d)).start())
        rdma(dn, 0, own, own, twin).start()
        loop(1, nz, lambda d: rdma(zn, d, own, low_z.at[n, z], zdev(d, c)).start())
        low_z[n, z] = field.astype(BF16)
        first()

        def forward(d):
            slot = low.at[n, c * np_ + plane_slot(d)]
            got(pn, d, slot)
            rdma(dn, d, slot, slot, twin).start()

        loop(1, np_, forward)
        loop(1, nz, lambda d: got(zn, d, low_z.at[n, zfrom(d)]))
        got(dn, 0, low.at[n, oc * np_ + p])
        loop(1, np_, lambda d: got(dn, d, low.at[n, oc * np_ + plane_slot(d)]))

        fields = jnp.concatenate([low[n, j] for j in range(2 * np_)], 1)

        def tile(k):
            t = lax.rem(lax.div(z, 2) + half // 2 + k, half)
            out = mm(fields, kern[t])
            for s in range(2):
                zz = 2 * t + s
                piece = out[:, s * B:(s + 1) * B]
                outb[n, zz] = piece
                each(zz, piece)

                @pl.when(zz != z)
                def _():
                    d = lax.rem(zz + nz - z, nz)
                    rdma(on, d, outb.at[n, zz], rcv.at[n, z], (x, zz, y, c)).start()

        loop(0, half, tile)
        last()
        rcv[n, z] = outb[n, z]
        loop(1, nz, lambda d: got(on, d, rcv.at[n, zfrom(d)]))
        total = rcv[n, 0]
        for zz in range(1, nz):
            total = total + rcv[n, zz]
        return total

    def z_start(name, buf, value):
        zc = 2 * z + c
        buf[zc] = value
        rdma(name + "_z", 0, buf.at[zc], buf.at[zc], twin).start()

        def go(d):
            rdma(name + "_z", 2 * d, buf.at[zc], buf.at[zc], zdev(d, c)).start()
            rdma(name + "_z", 2 * d + 1, buf.at[zc], buf.at[zc], zdev(d, oc)).start()

        loop(1, nz, go)

    def z_end(name, buf):
        got(name + "_z", 0, buf.at[2 * z + oc])

        def come(d):
            got(name + "_z", 2 * d, buf.at[2 * zfrom(d) + c])
            got(name + "_z", 2 * d + 1, buf.at[2 * zfrom(d) + oc])

        loop(1, nz, come)
        total = buf[0]
        for k in range(1, 2 * nz):
            total = total + buf[k]
        return total

    def p_start(name, buf, value):
        buf[p] = value
        loop(1, np_, lambda d: rdma(name + "_p", d, buf.at[p], buf.at[p], plane_dev(d)).start())

    def p_end(name, buf):
        loop(1, np_, lambda d: got(name + "_p", d, buf.at[plane_slot(d)]))
        total = buf[0]
        for k in range(1, np_):
            total = total + buf[k]
        return total

    def spread(row):
        return jnp.broadcast_to(row, (128, 128)).T

    def lane_sums(arrays):
        return jnp.sum(jnp.concatenate(arrays, 0).T, 0, keepdims=True)

    def none_yet():
        pass

    acc[...] = jnp.zeros_like(acc)

    def each0(zz, piece):
        acc[0] += piece * low_z[0, zz].astype(F32)

    def last0():
        r = rhs_s[1]
        p_start("cur0", cur_p.at[0], lane_sums([acc[0], r * r]))

    k0 = matvec(0, rhs, none_yet, each0, last0)
    z_start("cur0", cur_z.at[0], p_end("cur0", cur_p.at[0]))
    rhs = rhs_s[1]
    q1 = k0 + JITTER * rhs
    rhs_s[2] = k0
    sums = spread(z_end("cur0", cur_z.at[0]))
    m0 = sums[S:]
    alpha = m0 / (sums[:S] + JITTER * m0)
    r1 = rhs - alpha * q1
    rhs_s[3] = r1
    rhs_s[4] = alpha
    rhs_s[5] = m0

    acc[...] = jnp.zeros_like(acc)

    def first1():
        r, k, new = rhs_s[1], rhs_s[2], rhs_s[3]
        sums = lane_sums([new * new, new * r, new * k, r * k])
        z_start("mom", mom_z, jnp.concatenate([sums[:, :128], sums[:, 128:]], 0))

    def each1(zz, piece):
        acc[0] += piece * low_z[1, zz].astype(F32)
        acc[1] += piece * low_z[0, zz].astype(F32)

    def last1():
        p_start("cur1", cur_p.at[1], lane_sums([acc[0], acc[1]]))
        p_start("mom", mom_p, z_end("mom", mom_z))
        z_start("cur1", cur_z.at[1], p_end("cur1", cur_p.at[1]))

    k1 = matvec(1, r1, first1, each1, last1)
    prior, r, k0, r1, alpha, m0 = (rhs_s[k] for k in range(6))
    mom = p_end("mom", mom_p)
    one, two = spread(mom[0:1]), spread(mom[1:2])
    n1, r1r, r1k, rk = one[:S], one[S:], two[:S], two[S:]
    beta = n1 / m0
    kd = k1 + beta * k0
    dire = r1 + beta * r
    dd = n1 + beta * (2.0 * r1r + beta * m0)
    part = spread(z_end("cur1", cur_z.at[1]))
    curve = part[:S] + beta * part[S:] + beta * (r1k + beta * rk) + JITTER * dd
    alpha2 = n1 / curve
    post_ref[...] = prior + alpha * k0 + alpha2 * kd
    res_ref[...] = r1 - alpha2 * (kd + JITTER * dire)

    def sent(name, k, src):
        rdma(name, k, src, src, twin).wait_send()

    @pl.when(mine)
    def _():
        loop(1, nz, lambda d: sent("prm_z", d, prm_ref))

    def plane_sent(d):
        sent("prm_p", d, prm.at[p])
        sent("pts_p", d, pts_ref)
        sent("pts_d", d, pts_ref)
        for n in range(2):
            sent("low%d_p" % n, d, low.at[n, p])
            sent("low%d_d" % n, d, low.at[n, p])
            sent("cur%d_p" % n, d, cur_p.at[n, p])
        sent("mom_p", d, mom_p.at[p])

    loop(1, np_, plane_sent)
    sent("pts_d", 0, pts_ref)
    for n in range(2):
        sent("low%d_d" % n, 0, low.at[n, p])
        sent("cur%d_z" % n, 0, cur_z.at[n, z])
    sent("mom_z", 0, mom_z.at[z])

    def z_sent(d):
        sent("pts_z", d, pts_ref)
        for n in range(2):
            sent("low%d_z" % n, d, low.at[n, p])
            sent("out%d" % n, d, outb.at[n, z])
            for s in range(2):
                sent("cur%d_z" % n, 2 * d + s, cur_z.at[n, z])
        for s in range(2):
            sent("mom_z", 2 * d + s, mom_z.at[z])

    loop(1, nz, z_sent)


def body(sizes, points, targets, noise, omega, phase, weights):
    nx, nz, ny = sizes
    np_, half = nx * ny, nz // 2

    def cut(a):
        return lax.reduce_precision(a, 8, 7)

    turn = 1.0 / (2.0 * math.pi)
    parts = [weights]
    for v in (omega.T * turn, phase[:, None] * turn):
        one = cut(v)
        two = cut(v - one)
        parts.append((one, two, cut(v - one - two)))
    flat = [parts[0], *parts[1], *parts[2], jnp.zeros((FB, 128 - S - 3 * D - 3), F32)]
    packed = jnp.concatenate(flat, 1).astype(BF16)

    vmem = pl.BlockSpec(memory_space=pltpu.VMEM)
    sems = sum(count for _, count in SLOTS(nz, np_))
    block = jax.ShapeDtypeStruct((S, B), F32)
    return pl.pallas_call(
        functools.partial(kernel, sizes),
        out_shape=(block, block),
        in_specs=[vmem] * 4,
        out_specs=(vmem, vmem),
        scratch_shapes=[
            pltpu.VMEM((np_, half, FB, 128), BF16),
            pltpu.VMEM((2 * np_, D, B), F32),
            pltpu.VMEM((nz, D, B), F32),
            pltpu.VMEM((3, 128, 2 * B), BF16),
            pltpu.VMEM((S, 2 * B), F32),
            pltpu.VMEM((2, S, B), F32),
            pltpu.VMEM((6, S, B), F32),
            pltpu.VMEM((2, 2 * np_, S, B), BF16),
            pltpu.VMEM((2, nz, S, B), BF16),
            pltpu.VMEM((half, 64, 2 * B), BF16),
            pltpu.VMEM((half, 2 * np_ * B, 2 * B), BF16),
            pltpu.VMEM((2, nz, S, B), F32),
            pltpu.VMEM((3, nz, S, B), F32),
            pltpu.VMEM((2 * nz, 2, 128), F32),
            pltpu.VMEM((np_, 2, 128), F32),
            pltpu.VMEM((2, 2 * nz, 1, 128), F32),
            pltpu.VMEM((2, np_, 1, 128), F32),
            pltpu.SemaphoreType.DMA((sems,)),
            pltpu.SemaphoreType.DMA((sems,)),
        ],
        compiler_params=pltpu.CompilerParams(
            collective_id=0, has_side_effects=True, vmem_limit_bytes=40 * 1024 * 1024),
    )(points, targets[None, :], noise, packed)


def build(mesh, sizes):
    finer = Mesh(mesh.devices.reshape(*sizes, mesh.shape["cols"]), AXES)
    in_specs = (
        P(None, COLS_ROWS),
        P(COLS_ROWS),
        P(None, COLS_ROWS),
        P(None, ROWS),
        P(ROWS),
        P(ROWS, None),
    )
    out_specs = (P(None, COLS_ROWS), P(None, COLS_ROWS))
    return jax.shard_map(
        functools.partial(body, sizes), mesh=finer, in_specs=in_specs, out_specs=out_specs,
        check_vma=False)


def solution(mesh):
    return build(mesh, (4, 8, 4))
```

time: 663 us -> 75.2 us (0.11)
  blocking collectives: 380 us -> 0 us
  waiting for transfers between devices: 206 us -> 0 us
  Pallas kernels: 0 us -> 70.3 us
  matrix products: 55.4 us -> 0 us
  between operations: 13.8 us -> 0.68 us
    all_gather x1 -> x0, blocking collectives: 300 us -> none  [turned_gather(): lax.all_gather(both, axis, axis=0, tiled=True)]
    all_gather x3 -> x0, waiting for transfers between devices: 205 us -> none  [the longest x2 205 us: body(): lax.all_gather(low, ROWS_COLS, axis=1, tiled=True)]
    psum x8 -> x0, blocking collectives: 80.1 us -> none  [over_axes(): return functools.reduce(lax.psum, axes, value)]
    pallas_call x0 -> x1, Pallas kernels: none -> 70.3 us  [body(): pl.pallas_call(functools.partial(kernel, sizes), out_shape=(block, block)...]
    dot_general x5 -> x0, matrix products: 55.4 us -> none  [the longest x1 33.1 us: kernel_block(): lax.dot_general(left, right, (((0,), (0,)), ((), ())), precision=lax.Prec...]
  transfers between devices with their start and end apart: 3 -> 0, of which waited for: 2 -> 0; matrix products, arithmetic and copies ran while one was open for 7% -> 0% of each run, Pallas kernels for 0% -> 0%
where the time goes in v1:
time: 75.2 us; the launch traced here: 75 us
  Pallas kernels  70.3 us (93%)
  local copies, waits for them, and re-layouts  4.06 us (5%)
    pallas_call x1, Pallas kernels, body(): pl.pallas_call(functools.partial(kernel, sizes), out_shape=(block, block)...  70.3 us
    unnamed x15, local copies, waits for them, and re-layouts  3.67 us

profile of v1, /device:TPU:1, one launch (start us, length us, event | category | flops | bytes accessed | tf_op | source)
XLA Modules:
  0.0 75.0 jit_solution(8267646046871665582)
XLA Ops:
  0.6 0.0 copy-start.5
  0.6 0.6 copy-done.5
  1.3 0.0 copy-start.3
  1.3 0.1 copy.16
  1.4 0.1 copy.15
  1.5 0.1 copy.14
  1.6 0.4 copy-done.3
  2.0 0.0 copy-start.4
  2.0 0.7 copy-done.4
  2.7 0.1 copy.12
  2.8 0.0 copy-start
  2.8 0.0 copy-start.1
  2.8 0.0 copy-start.2
  2.8 0.1 concatenate.4.prm_ref
  2.9 0.6 copy-done
  3.5 0.0 copy-done.1
  3.5 0.0 copy-done.2
  3.5 70.3 %shard_map.77 = (f32[64,128]{1,0:T(8,128)S(1)}, f32[64,128]{1,0:T(8,128)S(1)}) custom-call(f32[8,128]{1,0:T(8,128)S(1)} %copy-done.1, f32[1,128]{1,0:T(1,128)S(1)} %bitcast.14, f32[64,128]{1,0:T(8,128)S(1)} %copy-done, bf16[16,128]{1,0:T(8,128)(2,1)S(1)} %concatenate.4.prm_ref), custom_call_target="tpu_custom_call" | custom-call | tf_op jit(solution)/shard_map/pallas_call | solution.py:450
  73.8 0.6 copy.19
  74.4 0.6 copy.20
  (4 shorter events, 0.0 us)
Async XLA Ops:
  0.6 0.7 copy-start.5
  1.3 0.7 copy-start.3
  2.0 0.7 copy-start.4
  2.8 0.8 %copy-start = (f32[64,128]{1,0:T(8,128)S(1)}, f32[64,128]{1,0:T(8,128)}, u32[]{:S(2)}) copy-start(f32[64,128]{1,0:T(8,128)} %noise_ref.1) | copy-start | bytes 98308
  2.8 0.7 copy-start.1
  2.8 0.7 copy-start.2

commit v2 on v0

v2 whole, which is shorter than its diff:
```python
import functools
import math

import jax
import jax.numpy as jnp
from jax import lax
from jax.experimental import pallas as pl
from jax.experimental.pallas import tpu as pltpu
from jax.sharding import Mesh
from jax.sharding import PartitionSpec as P

AXES = ("px", "pz", "py", "cols")
ROWS = ("px", "pz", "py")
COLS_ROWS = ("cols", "px", "pz", "py")
MESH = pl.DeviceIdType.MESH
F32, BF16 = jnp.float32, jnp.bfloat16

D = 8
S = 64
B = 128
FB = 16
JITTER = 0.25
KERN_EARLY = 10
SPREAD = math.sqrt(4.0 * math.log2(math.e))
SINE = [(-1) ** k * (2.0 * math.pi) ** (2 * k + 1) / math.factorial(2 * k + 1) for k in range(6)]


def SENDS():
    table = ["prm_z", "prm0", "prm1", "pts_z", "pts_p", "pts_d", "pts_o", "prior", "mom_z", "mom_p"]
    for n in "01":
        table += ["low%s_p" % n, "low%s_d" % n, "low%s_z" % n, "out%s" % n, "cur%s_z" % n, "cur%s_p" % n]
    return table


def RECVS(nx):
    several = {"prm_z": 4}
    for name in ("prm0", "prm1", "low0_p", "low0_d", "low1_p", "low1_d"):
        several[name] = nx
    return [(name, several.get(name, 1)) for name in SENDS()]


def three_parts(a):
    one = a.astype(BF16).astype(F32)
    rest = a - one
    two = rest.astype(BF16).astype(F32)
    three = (rest - two).astype(BF16).astype(F32)
    return one, two, three


def rows_of(pieces, width):
    row = lax.broadcasted_iota(jnp.int32, (8, width), 0)
    out = jnp.zeros((8, width), F32)
    for k, piece in enumerate(pieces):
        out = jnp.where(row == k, piece, out)
    return out


def exponent_left(points):
    scaled = points * SPREAD
    a1, a2, a3 = three_parts(scaled)
    n1, n2, n3 = three_parts(-0.5 * jnp.sum(scaled * scaled, 0, keepdims=True))
    width = points.shape[1]
    norms = rows_of((n1, n2, n3, 1.0, 1.0, 1.0), width)
    return jnp.concatenate([a1, a1, a2, a2, a1, a3, norms, jnp.zeros((8, width), F32)], 0)


def exponent_right(points):
    scaled = points * SPREAD
    b1, b2, b3 = three_parts(scaled)
    n1, n2, n3 = three_parts(-0.5 * jnp.sum(scaled * scaled, 0, keepdims=True))
    width = points.shape[1]
    norms = rows_of((1.0, 1.0, 1.0, n1, n2, n3), width)
    return jnp.concatenate([b1, b2, b1, b2, b3, b1, norms, jnp.zeros((8, width), F32)], 0)


def cos_turns(t):
    r = t - jnp.floor(t + 0.5)
    v = 0.25 - jnp.abs(r)
    w = v * v
    acc = jnp.full_like(w, SINE[-1])
    for c in SINE[-2::-1]:
        acc = acc * w + c
    return acc * v


def mm(a, b, dims=(((1,), (0,)), ((), ()))):
    return lax.dot_general(a, b, dims, preferred_element_type=F32)


def kernel(
    sizes,
    pts_hbm, tgt_hbm, noise_hbm, omega_hbm, phase_hbm, weights_hbm,
    post_ref, res_ref,
    pts, tgt, noise, omega, phase, weights,
    prm_own, bundle, ptw, ptsj, ptsi, pside, prior_s, halves, acc, rhs_s, low, low_z, right, kern, outb, rcv,
    mom_z, mom_p, cur_z, cur_p, send, recv, local,
):
    nx, nz, ny = sizes
    np_, half = nx * ny, nz // 2
    nfeat = nx * nz * ny * FB
    x, z, y, c = (lax.axis_index(a) for a in AXES)
    xs = [x] + [lax.rem(x + d, nx) for d in range(1, nx)]
    ys = [y] + [lax.rem(y + d, ny) for d in range(1, ny)]
    zs = [z] + [lax.rem(z + d, nz) for d in range(1, nz)]
    p = x * ny + y
    oc = 1 - c
    twin = (x, z, y, oc)

    arrivals = []
    for k, (src, dst) in enumerate((
        (weights_hbm, weights), (omega_hbm, omega), (phase_hbm, phase), (pts_hbm, pts),
        (tgt_hbm, tgt), (noise_hbm, noise),
    )):
        copy = pltpu.make_async_copy(src, dst, local.at[k])
        copy.start()
        arrivals.append(copy)

    at = {}
    top = 0
    for name, count in RECVS(nx):
        at[name] = top
        top += count
    order = {name: k for k, name in enumerate(SENDS())}

    def rdma(name, k, src, dst, dev):
        return pltpu.make_async_remote_copy(
            src_ref=src, dst_ref=dst, send_sem=send.at[order[name]], recv_sem=recv.at[at[name] + k],
            device_id=dev, device_id_type=MESH)

    pending = []

    def put(name, k, src, dst, dev):
        rdma(name, k, src, dst, dev).start()

    def sent(name, whole):
        pending.append((name, whole))

    def flush():
        for name, whole in pending:
            rdma(name, 0, whole, whole, twin).wait_send()
        pending.clear()

    def got(name, k, dst):
        rdma(name, k, dst, dst, twin).wait_recv()

    def hops(d, n):
        return min(d, n - d)

    def dxy(d):
        return d // ny, d % ny

    near_p = sorted(range(1, np_), key=lambda d: hops(d // ny, nx) + hops(d % ny, ny))
    far_p = near_p[::-1]
    near_z = sorted(range(1, nz), key=lambda d: hops(d, nz))
    far_z = near_z[::-1]

    def plane_dev(d):
        dx, dy = dxy(d)
        return (xs[dx], z, ys[dy], c)

    def plane_slot(d):
        dx, dy = dxy(d)
        return xs[(nx - dx) % nx] * ny + ys[(ny - dy) % ny]

    def zdev(d, core):
        return (x, zs[d], y, core)

    def zfrom(d):
        return zs[(nz - d) % nz]

    with jax.named_scope("a_barrier"):
        bar = pltpu.get_barrier_semaphore()

        def greet(dev):
            pl.semaphore_signal(bar, inc=1, device_id=dev, device_id_type=MESH)

        for d in far_p:
            greet(plane_dev(d))
        for d in far_z:
            greet(zdev(d, c))
            greet(zdev(d, oc))
        greet(twin)

        turn = 1.0 / (2.0 * math.pi)
        for copy in arrivals[:4]:
            copy.wait()
        lane = lax.broadcasted_iota(jnp.int32, (FB, 128), 1)
        row = lax.broadcasted_iota(jnp.int32, (FB, 128), 0)
        angles = jnp.concatenate([omega[...], phase[...], jnp.zeros((FB - D - 1, FB), F32)], 0) * turn
        packed = jnp.zeros((FB, 128), F32)
        flip = (((0,), (0,)), ((), ()))
        for k, piece in enumerate(three_parts(angles)):
            spot = jnp.where(row < D, S + k * D + row, S + 3 * D + k)
            pick = jnp.where((lane == spot) & (row <= D), 1.0, 0.0)
            packed = packed + mm(piece.astype(BF16), pick.astype(BF16), flip)
        w1 = weights[...].astype(BF16)
        w2 = (weights[...] - w1.astype(F32)).astype(BF16)
        wide = lax.broadcasted_iota(jnp.int32, (S, 128), 1)
        deep = lax.broadcasted_iota(jnp.int32, (S, 128), 0)
        once = jnp.where(wide == deep, 1.0, 0.0).astype(BF16)
        twice = jnp.where((wide == deep) | (wide == deep + S), 1.0, 0.0).astype(BF16)
        prm_own[0] = (packed + mm(w1, once)).astype(BF16)
        prm_own[1] = mm(w2, twice).astype(BF16)
        pl.semaphore_wait(bar, 1 + 2 * (nz - 1) + np_ - 1)

    mine = lax.rem(z, 2) == c
    zslot = lax.div(z, 2)

    with jax.named_scope("b_prm_z"):
        par = lax.rem(z + c, 2)
        turnout = {1: 0, 7: 1, 3: 2, 5: 3, 2: 1, 6: 2, 4: 3}
        places = [par, 2 + 5 * par, 6 - 3 * par, 4 + par]

        @pl.when(mine)
        def _():
            for d in far_z:
                put("prm_z", turnout[d], prm_own, halves.at[d], zdev(d, c))
            halves[0] = prm_own[...]

        put("pts_o", 0, pts, ptw, twin)
        sent("pts_o", pts)
        for d in far_p:
            put("pts_p", 0, pts, ptsj.at[c * np_ + p], plane_dev(d))
        for d in far_z:
            put("pts_z", 0, pts, ptsi.at[z], zdev(d, c))
        sent("pts_p", ptsj.at[pl.ds(0, np_ - 1)])
        sent("pts_z", ptsi.at[pl.ds(0, nz - 1)])
        ptsj[c * np_ + p] = pts[...]
        ptsi[z] = pts[...]

        left_lanes = lax.broadcasted_iota(jnp.int32, (FB, 128), 1) < S
        for stage in range(2):
            if stage == 0:
                @pl.when(jnp.logical_not(mine))
                def _():
                    got("prm_z", 0, halves.at[1])
            else:
                got("prm_z", 2, halves.at[places[2]])
            got("prm_z", 2 * stage + 1, halves.at[places[2 * stage + 1]])
            one, two = halves[places[2 * stage]], halves[places[2 * stage + 1]]
            bundle[stage, p, 0] = one[0]
            bundle[stage, p, 1] = two[0]
            bundle[stage, p, 2] = jnp.where(left_lanes, one[1].astype(F32), two[1].astype(F32)).astype(BF16)
            name = "prm%d" % stage
            for d in far_p:
                put(name, d // ny, bundle.at[stage, p], bundle.at[stage, p], plane_dev(d))
            sent(name, bundle.at[stage, pl.ds(0, np_ - 1)])

    with jax.named_scope("c_points"):
        got("pts_o", 0, ptw)
        got("pts_p", 0, ptsj.at[pl.ds(0, np_ - 1)])
        here = ptsj.at[pl.ds(c * np_, np_)]
        put("pts_d", 0, here, here, twin)
        sent("pts_d", here)
        got("pts_z", 0, ptsi.at[pl.ds(0, nz - 1)])
        both = jnp.concatenate([pts[...], ptw[...]], 1)
        b1, b2, b3 = three_parts(both)
        none = jnp.zeros((S, 2 * B), F32)
        ones = rows_of((1.0, 1.0, 1.0), 2 * B)
        pside[0] = jnp.concatenate([none, b1, b1, b1, ones, none[:32]], 0).astype(BF16)
        pside[1] = jnp.concatenate([none, b2, b2, none[:48]], 0).astype(BF16)
        pside[2] = jnp.concatenate([none, b3, none[:56]], 0).astype(BF16)
        prior_s[...] = jnp.zeros_like(prior_s)
        for t in range(half):
            two = jnp.concatenate([ptsi[2 * t], ptsi[2 * t + 1]], 1)
            right[t] = exponent_right(two).astype(BF16)
        got("pts_d", 0, ptsj.at[pl.ds(oc * np_, np_)])

    def kern_block(j, carry):
        two = jnp.concatenate([ptsj[2 * j], ptsj[2 * j + 1]], 1)
        left = exponent_left(two).T.astype(BF16)
        row = pl.multiple_of(j * 2 * B, 2 * B)
        for t in range(half):
            kern[t, pl.ds(row, 2 * B), :] = jnp.exp2(mm(left, right[t])).astype(BF16)
        return carry

    early = (np_ * KERN_EARLY) // 16
    with jax.named_scope("d_kern"):
        lax.fori_loop(0, early, kern_block, 0)

    with jax.named_scope("e_prior"):
        for dx in sorted(range(nx), key=lambda d: hops(d, nx)):
            base = xs[(nx - dx) % nx] * ny
            for stage in range(2):
                group = bundle.at[stage, pl.ds(0, ny - 1)] if dx == 0 else bundle.at[stage, pl.ds(base, ny)]
                got("prm%d" % stage, dx, group)
                part = jnp.concatenate([bundle[stage, base + q, k] for k in range(2) for q in range(ny)], 0)
                rest = jnp.concatenate([bundle[stage, base + q, 2] for q in range(ny)], 0)
                cut = ny * FB
                turns = mm(part, pside[0]) + mm(part, pside[1]) + mm(part, pside[2])
                feats = cos_turns(turns)
                f1 = feats.astype(BF16)
                f2 = (feats - f1.astype(F32)).astype(BF16)
                total = (mm(part, f1, flip) + mm(part, f2, flip))[:S]
                prior_s[...] += total + mm(rest, f1[:cut], flip)[:S] + mm(rest, f1[cut:], flip)[S:]

    with jax.named_scope("f_swap"):
        rcv[2, 1] = prior_s[:, B:]
        put("prior", 0, rcv.at[2, 1], rcv.at[2, 0], twin)
        sent("prior", rcv.at[2, 1])
        for copy in arrivals[4:]:
            copy.wait()
        got("prior", 0, rcv.at[2, 0])
        scale = math.sqrt(2.0 / nfeat)
        prior = scale * (prior_s[:, :B] + rcv[2, 0])
        rhs = tgt[...] - prior - 0.5 * noise[...]
        rhs_s[0] = prior
        rhs_s[1] = rhs
        low[0, c * np_ + p] = rhs.astype(BF16)
        low_z[0, z] = rhs.astype(BF16)

    def matvec(n, first, each, last):
        pn, dn, zn, on = "low%d_p" % n, "low%d_d" % n, "low%d_z" % n, "out%d" % n
        own = low.at[n, c * np_ + p]
        with jax.named_scope("g%d_send" % n):
            for d in far_p:
                put(pn, d // ny, own, own, plane_dev(d))
            for d in far_z:
                put(zn, 0, own, low_z.at[n, z], zdev(d, c))
            sent(pn, low.at[n, pl.ds(0, np_ - 1)])
            sent(zn, low_z.at[n, pl.ds(0, nz - 1)])
            sent(dn, low.at[n, pl.ds(0, np_)])
        with jax.named_scope("h%d_first" % n):
            first()

        def group_of(core, dx):
            return low.at[n, pl.ds(core * np_ + xs[(nx - dx) % nx] * ny, ny)]

        def own_group(dx):
            group = group_of(c, dx)
            got(pn, dx, low.at[n, pl.ds(0, ny - 1)] if dx == 0 else group)
            put(dn, dx, group, group, twin)

        def twin_group(dx):
            got(dn, dx, group_of(oc, dx))

        def times(core, dx, t):
            base = core * np_ + xs[(nx - dx) % nx] * ny
            fields = jnp.concatenate([low[n, base + q] for q in range(ny)], 1)
            row = pl.multiple_of(base * B, B * ny)
            return mm(fields, kern[t, pl.ds(row, B * ny), :])

        def add_tiles(groups, fresh):
            def tile(t, carry):
                out = times(*groups[0], t)
                for group in groups[1:]:
                    out = out + times(*group, t)
                for s in range(2):
                    piece = out[:, s * B:(s + 1) * B]
                    zz = 2 * t + s
                    outb[n, zz] = piece if fresh else outb[n, zz] + piece
                return carry

            lax.fori_loop(0, half, tile, 0)

        spans = sorted(range(nx), key=lambda d: hops(d, nx))
        with jax.named_scope("i%d_gather" % n):
            own_group(spans[0])
            own_group(spans[1])
            add_tiles([(c, spans[0]), (c, spans[1])], True)
            own_group(spans[2])
            got(zn, 0, low_z.at[n, pl.ds(0, nz - 1)])
            twin_group(spans[0])
            twin_group(spans[1])
            add_tiles([(oc, spans[0]), (oc, spans[1])], False)
            own_group(spans[3])
            twin_group(spans[2])
            add_tiles([(c, spans[2]), (c, spans[3]), (oc, spans[2])], False)
            twin_group(spans[3])
            flush()

        with jax.named_scope("j%d_tiles" % n):
            for k in range(half):
                t = lax.rem(zslot + half // 2 + k, half)
                out = times(oc, spans[3], t)
                for s in range(2):
                    zz = 2 * t + s
                    piece = outb[n, zz] + out[:, s * B:(s + 1) * B]
                    outb[n, zz] = piece
                    each(zz, piece)
                if k == half - half // 2 or half == 1:
                    targets = [z + 1 - 2 * lax.rem(z, 2)]
                else:
                    targets = [2 * t, 2 * t + 1]
                for zz in targets:
                    put(on, 0, outb.at[n, zz], rcv.at[n, z], (x, zz, y, c))
            sent(on, outb.at[n, pl.ds(0, nz - 1)])
        with jax.named_scope("k%d_last" % n):
            last()
        with jax.named_scope("l%d_reduce" % n):
            total = outb[n, z]
            got(on, 0, rcv.at[n, pl.ds(0, nz - 1)])
            for d in near_z:
                total = total + rcv[n, zfrom(d)]
        return total

    def z_start(name, buf, value):
        zc = 2 * z + c
        buf[zc] = value
        for d in far_z:
            put(name + "_z", 0, buf.at[zc], buf.at[zc], zdev(d, c))
            put(name + "_z", 0, buf.at[zc], buf.at[zc], zdev(d, oc))
        put(name + "_z", 0, buf.at[zc], buf.at[zc], twin)
        sent(name + "_z", buf.at[pl.ds(0, 2 * nz - 1)])

    def z_end(name, buf):
        got(name + "_z", 0, buf.at[pl.ds(0, 2 * nz - 1)])
        return sum_all(buf, 2 * nz)

    def p_start(name, buf, value):
        buf[p] = value
        for d in far_p:
            put(name + "_p", 0, buf.at[p], buf.at[p], plane_dev(d))
        sent(name + "_p", buf.at[pl.ds(0, np_ - 1)])

    def p_end(name, buf):
        got(name + "_p", 0, buf.at[pl.ds(0, np_ - 1)])
        return sum_all(buf, np_)

    def sum_all(buf, count):
        parts = [buf[k] for k in range(count)]
        while len(parts) > 1:
            parts = [a + b for a, b in zip(parts[::2], parts[1::2])]
        return parts[0]

    def spread(row):
        return jnp.broadcast_to(row, (128, 128)).T

    def lane_sums(arrays):
        return jnp.sum(jnp.concatenate(arrays, 0).T, 0, keepdims=True)

    acc[...] = jnp.zeros_like(acc)

    def first0():
        lax.fori_loop(early, np_, kern_block, 0)

    def each0(zz, piece):
        acc[0] += piece * low_z[0, zz].astype(F32)

    def last0():
        r = rhs_s[1]
        p_start("cur0", cur_p.at[0], lane_sums([acc[0], r * r]))
        z_start("cur0", cur_z.at[0], p_end("cur0", cur_p.at[0]))

    k0 = matvec(0, first0, each0, last0)
    with jax.named_scope("m_alpha"):
        rhs = rhs_s[1]
        q1 = k0 + JITTER * rhs
        rhs_s[2] = k0
        acc[...] = jnp.zeros_like(acc)
        sums = spread(z_end("cur0", cur_z.at[0]))
        m0 = sums[S:]
        alpha = m0 / (sums[:S] + JITTER * m0)
        r1 = rhs - alpha * q1
        low[1, c * np_ + p] = r1.astype(BF16)
        low_z[1, z] = r1.astype(BF16)
        rhs_s[3] = r1
        rhs_s[4] = alpha
        rhs_s[5] = m0

    def first1():
        r, k, new = rhs_s[1], rhs_s[2], rhs_s[3]
        sums = lane_sums([new * new, new * r, new * k, r * k])
        z_start("mom", mom_z, jnp.concatenate([sums[:, :128], sums[:, 128:]], 0))

    def each1(zz, piece):
        acc[0] += piece * low_z[1, zz].astype(F32)
        acc[1] += piece * low_z[0, zz].astype(F32)

    def last1():
        p_start("cur1", cur_p.at[1], lane_sums([acc[0], acc[1]]))
        p_start("mom", mom_p, z_end("mom", mom_z))
        z_start("cur1", cur_z.at[1], p_end("cur1", cur_p.at[1]))

    k1 = matvec(1, first1, each1, last1)
    with jax.named_scope("n_finish"):
        prior, r, k0, r1, alpha, m0 = (rhs_s[k] for k in range(6))
        mom = p_end("mom", mom_p)
        one, two = spread(mom[0:1]), spread(mom[1:2])
        n1, r1r, r1k, rk = one[:S], one[S:], two[:S], two[S:]
        beta = n1 / m0
        kd = k1 + beta * k0
        dire = r1 + beta * r
        dd = n1 + beta * (2.0 * r1r + beta * m0)
        known = beta * (r1k + beta * rk) + JITTER * dd
        part = spread(z_end("cur1", cur_z.at[1]))
        alpha2 = n1 / (part[:S] + beta * part[S:] + known)
        post_ref[...] = prior + alpha * k0 + alpha2 * kd
        res_ref[...] = r1 - alpha2 * (kd + JITTER * dire)

        flush()

        @pl.when(mine)
        def _():
            whole = halves.at[pl.ds(0, nz - 1)]
            rdma("prm_z", 0, whole, whole, twin).wait_send()


def body(sizes, points, targets, noise, omega, phase, weights):
    nx, nz, ny = sizes
    np_, half = nx * ny, nz // 2
    vmem = pl.BlockSpec(memory_space=pltpu.VMEM)
    hbm = pl.BlockSpec(memory_space=pltpu.HBM)
    block = pltpu.VMEM((S, B), F32)
    return pl.pallas_call(
        functools.partial(kernel, sizes),
        out_shape=(block, block),
        in_specs=[hbm] * 6,
        out_specs=(vmem, vmem),
        scratch_shapes=[
            pltpu.VMEM((D, B), F32),
            pltpu.VMEM((1, B), F32),
            pltpu.VMEM((S, B), F32),
            pltpu.VMEM((D, FB), F32),
            pltpu.VMEM((1, FB), F32),
            pltpu.VMEM((FB, S), F32),
            pltpu.VMEM((2, FB, 128), BF16),
            pltpu.VMEM((2, np_, 3, FB, 128), BF16),
            pltpu.VMEM((D, B), F32),
            pltpu.VMEM((2 * np_, D, B), F32),
            pltpu.VMEM((nz, D, B), F32),
            pltpu.VMEM((3, 128, 2 * B), BF16),
            pltpu.VMEM((S, 2 * B), F32),
            pltpu.VMEM((nz, 2, FB, 128), BF16),
            pltpu.VMEM((2, S, B), F32),
            pltpu.VMEM((6, S, B), F32),
            pltpu.VMEM((2, 2 * np_, S, B), BF16),
            pltpu.VMEM((2, nz, S, B), BF16),
            pltpu.VMEM((half, 64, 2 * B), BF16),
            pltpu.VMEM((half, 2 * np_ * B, 2 * B), BF16),
            pltpu.VMEM((2, nz, S, B), F32),
            pltpu.VMEM((3, nz, S, B), F32),
            pltpu.VMEM((2 * nz, 2, 128), F32),
            pltpu.VMEM((np_, 2, 128), F32),
            pltpu.VMEM((2, 2 * nz, 1, 128), F32),
            pltpu.VMEM((2, np_, 1, 128), F32),
            pltpu.SemaphoreType.DMA((len(SENDS()),)),
            pltpu.SemaphoreType.DMA((sum(count for _, count in RECVS(nx)),)),
            pltpu.SemaphoreType.DMA((6,)),
        ],
        compiler_params=pltpu.CompilerParams(
            collective_id=0, has_side_effects=True, vmem_limit_bytes=62000000),
    )(points, targets[None, :], noise, omega, phase[None, :], weights)


def build(mesh, sizes):
    finer = Mesh(mesh.devices.reshape(*sizes, mesh.shape["cols"]), AXES)
    in_specs = (
        P(None, COLS_ROWS),
        P(COLS_ROWS),
        P(None, COLS_ROWS),
        P(None, ROWS),
        P(ROWS),
        P(ROWS, None),
    )
    out_specs = (P(None, COLS_ROWS), P(None, COLS_ROWS))
    return jax.shard_map(
        functools.partial(body, sizes), mesh=finer, in_specs=in_specs, out_specs=out_specs,
        check_vma=False)


def solution(mesh):
    return build(mesh, (4, 8, 4))
```

time: 663 us -> 64.9 us (0.10)
  blocking collectives: 380 us -> 0 us
  waiting for transfers between devices: 206 us -> 0 us
  Pallas kernels: 0 us -> 62.8 us
  matrix products: 55.4 us -> 0 us
  between operations: 13.8 us -> 0.64 us
    all_gather x1 -> x0, blocking collectives: 300 us -> none  [turned_gather(): lax.all_gather(both, axis, axis=0, tiled=True)]
    all_gather x3 -> x0, waiting for transfers between devices: 205 us -> none  [the longest x2 205 us: body(): lax.all_gather(low, ROWS_COLS, axis=1, tiled=True)]
    psum x8 -> x0, blocking collectives: 80.1 us -> none  [over_axes(): return functools.reduce(lax.psum, axes, value)]
    pallas_call x0 -> x1, Pallas kernels: none -> 62.8 us  [body(): pl.pallas_call(functools.partial(kernel, sizes), out_shape=(block, block)...]
    dot_general x5 -> x0, matrix products: 55.4 us -> none  [the longest x1 33.1 us: kernel_block(): lax.dot_general(left, right, (((0,), (0,)), ((), ())), precision=lax.Prec...]
  transfers between devices with their start and end apart: 3 -> 0, of which waited for: 2 -> 0; matrix products, arithmetic and copies ran while one was open for 7% -> 0% of each run, Pallas kernels for 0% -> 0%
where the time goes in v2:
time: 64.9 us; the launch traced here: 64.7 us
  Pallas kernels  62.8 us (97%)
  local copies, waits for them, and re-layouts  1.23 us (2%)
    pallas_call x1, Pallas kernels, body(): pl.pallas_call(functools.partial(kernel, sizes), out_shape=(block, block)...  62.8 us

profile of v2, /device:TPU:1, one launch (start us, length us, event | category | flops | bytes accessed | tf_op | source)
XLA Modules:
  0.0 64.7 jit_solution(15628142277280941951)
XLA Ops:
  0.6 62.8 %shard_map.77 = (f32[64,128]{1,0:T(8,128)S(1)}, f32[64,128]{1,0:T(8,128)S(1)}) custom-call(f32[8,128]{1,0:T(8,128)} %pts_hbm.1, f32[1,128]{1,0:T(1,128)} %bitcast.2, f32[64,128]{1,0:T(8,128)} %noise_hbm.1, f32[8,16]{1,0:T(8,128)} %omega_hbm.1, f32[1,16]{1,0:T(1,128)} %bitcast.3, f32[16,64]{1,0:T(8,128)} %weights_hbm.1), custom_call_target="tpu_custom_call" | custom-call | tf_op jit(solution)/shard_map/pallas_call | solution.py:505
  63.5 0.6 copy.10
  64.1 0.6 copy.11

commit v3 on v2

--- a/solution.py
+++ b/solution.py
@@ -20,7 +20,7 @@
 B = 128
 FB = 16
 JITTER = 0.25
-KERN_EARLY = 10
+KERN_EARLY = 7
 SPREAD = math.sqrt(4.0 * math.log2(math.e))
 SINE = [(-1) ** k * (2.0 * math.pi) ** (2 * k + 1) / math.factorial(2 * k + 1) for k in range(6)]
 
@@ -90,9 +90,9 @@
 def kernel(
     sizes,
     pts_hbm, tgt_hbm, noise_hbm, omega_hbm, phase_hbm, weights_hbm,
-    post_ref, res_ref,
+    out_ref,
     pts, tgt, noise, omega, phase, weights,
-    prm_own, bundle, ptw, ptsj, ptsi, pside, prior_s, halves, acc, rhs_s, low, low_z, right, kern, outb, rcv,
+    prm_own, bundle, ptw, ptsj, ptsi, pside, prior_s, halves, rhs_s, low, low_z, right, kern, outb, rcv,
     mom_z, mom_p, cur_z, cur_p, send, recv, local,
 ):
     nx, nz, ny = sizes
@@ -279,14 +279,19 @@
         lax.fori_loop(0, early, kern_block, 0)
 
     with jax.named_scope("e_prior"):
-        for dx in sorted(range(nx), key=lambda d: hops(d, nx)):
-            base = xs[(nx - dx) % nx] * ny
-            for stage in range(2):
+        spans = sorted(range(nx), key=lambda d: hops(d, nx))
+        for stage in range(2):
+            columns = []
+            for dx in spans:
+                base = xs[(nx - dx) % nx] * ny
                 group = bundle.at[stage, pl.ds(0, ny - 1)] if dx == 0 else bundle.at[stage, pl.ds(base, ny)]
                 got("prm%d" % stage, dx, group)
-                part = jnp.concatenate([bundle[stage, base + q, k] for k in range(2) for q in range(ny)], 0)
-                rest = jnp.concatenate([bundle[stage, base + q, 2] for q in range(ny)], 0)
-                cut = ny * FB
+                columns.append(base)
+            for bases in (columns[:2], columns[2:]):
+                pick = [(base + q, k) for k in range(2) for base in bases for q in range(ny)]
+                part = jnp.concatenate([bundle[stage, slot, k] for slot, k in pick], 0)
+                rest = jnp.concatenate([bundle[stage, base + q, 2] for base in bases for q in range(ny)], 0)
+                cut = rest.shape[0]
                 turns = mm(part, pside[0]) + mm(part, pside[1]) + mm(part, pside[2])
                 feats = cos_turns(turns)
                 f1 = feats.astype(BF16)
@@ -341,7 +346,7 @@
             return mm(fields, kern[t, pl.ds(row, B * ny), :])
 
         def add_tiles(groups, fresh):
-            def tile(t, carry):
+            for t in range(half):
                 out = times(*groups[0], t)
                 for group in groups[1:]:
                     out = out + times(*group, t)
@@ -349,44 +354,41 @@
                     piece = out[:, s * B:(s + 1) * B]
                     zz = 2 * t + s
                     outb[n, zz] = piece if fresh else outb[n, zz] + piece
-                return carry
-
-            lax.fori_loop(0, half, tile, 0)
 
         spans = sorted(range(nx), key=lambda d: hops(d, nx))
-        with jax.named_scope("i%d_gather" % n):
+        with jax.named_scope("i%d_gather_a" % n):
             own_group(spans[0])
             own_group(spans[1])
+        with jax.named_scope("i%d_gather_b" % n):
             add_tiles([(c, spans[0]), (c, spans[1])], True)
+        with jax.named_scope("i%d_gather_c" % n):
             own_group(spans[2])
+            own_group(spans[3])
+            twin_group(spans[0])
+        with jax.named_scope("i%d_gather_d" % n):
+            add_tiles([(c, spans[2]), (c, spans[3]), (oc, spans[0])], False)
+        with jax.named_scope("i%d_gather_e" % n):
             got(zn, 0, low_z.at[n, pl.ds(0, nz - 1)])
-            twin_group(spans[0])
             twin_group(spans[1])
-            add_tiles([(oc, spans[0]), (oc, spans[1])], False)
-            own_group(spans[3])
             twin_group(spans[2])
-            add_tiles([(c, spans[2]), (c, spans[3]), (oc, spans[2])], False)
             twin_group(spans[3])
             flush()
 
         with jax.named_scope("j%d_tiles" % n):
-            for k in range(half):
-                t = lax.rem(zslot + half // 2 + k, half)
-                out = times(oc, spans[3], t)
+            sums = None
+            for t in range(half):
+                out = times(oc, spans[1], t) + times(oc, spans[2], t) + times(oc, spans[3], t)
                 for s in range(2):
                     zz = 2 * t + s
                     piece = outb[n, zz] + out[:, s * B:(s + 1) * B]
                     outb[n, zz] = piece
-                    each(zz, piece)
-                if k == half - half // 2 or half == 1:
-                    targets = [z + 1 - 2 * lax.rem(z, 2)]
-                else:
-                    targets = [2 * t, 2 * t + 1]
-                for zz in targets:
-                    put(on, 0, outb.at[n, zz], rcv.at[n, z], (x, zz, y, c))
+                    terms = each(zz, piece)
+                    sums = terms if sums is None else [a + b for a, b in zip(sums, terms)]
+            for d in far_z:
+                put(on, 0, outb.at[n, zs[d]], rcv.at[n, z], zdev(d, c))
             sent(on, outb.at[n, pl.ds(0, nz - 1)])
         with jax.named_scope("k%d_last" % n):
-            last()
+            last(sums)
         with jax.named_scope("l%d_reduce" % n):
             total = outb[n, z]
             got(on, 0, rcv.at[n, pl.ds(0, nz - 1)])
@@ -429,17 +431,15 @@
     def lane_sums(arrays):
         return jnp.sum(jnp.concatenate(arrays, 0).T, 0, keepdims=True)
 
-    acc[...] = jnp.zeros_like(acc)
-
     def first0():
         lax.fori_loop(early, np_, kern_block, 0)
 
     def each0(zz, piece):
-        acc[0] += piece * low_z[0, zz].astype(F32)
-
-    def last0():
+        return [piece * low_z[0, zz].astype(F32)]
+
+    def last0(sums):
         r = rhs_s[1]
-        p_start("cur0", cur_p.at[0], lane_sums([acc[0], r * r]))
+        p_start("cur0", cur_p.at[0], lane_sums([*sums, r * r]))
         z_start("cur0", cur_z.at[0], p_end("cur0", cur_p.at[0]))
 
     k0 = matvec(0, first0, each0, last0)
@@ -447,7 +447,6 @@
         rhs = rhs_s[1]
         q1 = k0 + JITTER * rhs
         rhs_s[2] = k0
-        acc[...] = jnp.zeros_like(acc)
         sums = spread(z_end("cur0", cur_z.at[0]))
         m0 = sums[S:]
         alpha = m0 / (sums[:S] + JITTER * m0)
@@ -464,11 +463,10 @@
         z_start("mom", mom_z, jnp.concatenate([sums[:, :128], sums[:, 128:]], 0))
 
     def each1(zz, piece):
-        acc[0] += piece * low_z[1, zz].astype(F32)
-        acc[1] += piece * low_z[0, zz].astype(F32)
-
-    def last1():
-        p_start("cur1", cur_p.at[1], lane_sums([acc[0], acc[1]]))
+        return [piece * low_z[1, zz].astype(F32), piece * low_z[0, zz].astype(F32)]
+
+    def last1(sums):
+        p_start("cur1", cur_p.at[1], lane_sums(sums))
         p_start("mom", mom_p, z_end("mom", mom_z))
         z_start("cur1", cur_z.at[1], p_end("cur1", cur_p.at[1]))
 
@@ -485,8 +483,8 @@
         known = beta * (r1k + beta * rk) + JITTER * dd
         part = spread(z_end("cur1", cur_z.at[1]))
         alpha2 = n1 / (part[:S] + beta * part[S:] + known)
-        post_ref[...] = prior + alpha * k0 + alpha2 * kd
-        res_ref[...] = r1 - alpha2 * (kd + JITTER * dire)
+        out_ref[:S] = prior + alpha * k0 + alpha2 * kd
+        out_ref[S:] = r1 - alpha2 * (kd + JITTER * dire)
 
         flush()
 
@@ -501,12 +499,12 @@
     np_, half = nx * ny, nz // 2
     vmem = pl.BlockSpec(memory_space=pltpu.VMEM)
     hbm = pl.BlockSpec(memory_space=pltpu.HBM)
-    block = pltpu.VMEM((S, B), F32)
-    return pl.pallas_call(
+    block = pltpu.VMEM((2 * S, B), F32)
+    both = pl.pallas_call(
         functools.partial(kernel, sizes),
-        out_shape=(block, block),
+        out_shape=block,
         in_specs=[hbm] * 6,
-        out_specs=(vmem, vmem),
+        out_specs=vmem,
         scratch_shapes=[
             pltpu.VMEM((D, B), F32),
             pltpu.VMEM((1, B), F32),
@@ -522,7 +520,6 @@
             pltpu.VMEM((3, 128, 2 * B), BF16),
             pltpu.VMEM((S, 2 * B), F32),
             pltpu.VMEM((nz, 2, FB, 128), BF16),
-            pltpu.VMEM((2, S, B), F32),
             pltpu.VMEM((6, S, B), F32),
             pltpu.VMEM((2, 2 * np_, S, B), BF16),
             pltpu.VMEM((2, nz, S, B), BF16),
@@ -541,6 +538,7 @@
         compiler_params=pltpu.CompilerParams(
             collective_id=0, has_side_effects=True, vmem_limit_bytes=62000000),
     )(points, targets[None, :], noise, omega, phase[None, :], weights)
+    return both[:S], both[S:]
 
 
 def build(mesh, sizes):

time: 64.9 us -> 59.5 us (0.917)
  Pallas kernels: 62.8 us -> 58.1 us
    pallas_call x1, Pallas kernels: 62.8 us -> 58.1 us  [body(): pl.pallas_call(functools.partial(kernel, sizes), out_shape=block, in_spec...]
    unnamed x2 -> x0, local copies, waits for them, and re-layouts: 1.23 us -> none
where the time goes in v3:
time: 59.5 us; the launch traced here: 59.3 us
  Pallas kernels  58.1 us (98%)
  between operations  0.64 us (1%)
  local copies, waits for them, and re-layouts  0.63 us (1%)
    pallas_call x1, Pallas kernels, body(): pl.pallas_call(functools.partial(kernel, sizes), out_shape=block, in_spec...  58.1 us

profile of v3, /device:TPU:1, one launch (start us, length us, event | category | flops | bytes accessed | tf_op | source)
XLA Modules:
  0.0 59.3 jit_solution(15463631049250346259)
XLA Ops:
  0.6 58.1 %shard_map.77 = f32[128,128]{1,0:T(8,128)S(1)} custom-call(f32[8,128]{1,0:T(8,128)} %pts_hbm.1, f32[1,128]{1,0:T(1,128)} %bitcast.2, f32[64,128]{1,0:T(8,128)} %noise_hbm.1, f32[8,16]{1,0:T(8,128)} %omega_hbm.1, f32[1,16]{1,0:T(1,128)} %bitcast.3, f32[16,64]{1,0:T(8,128)} %weights_hbm.1), custom_call_target="tpu_custom_call" | custom-call | tf_op jit(solution)/shard_map/pallas_call | solution.py:503
  58.7 0.6 %fusion = (f32[64,128]{1,0:T(8,128)}, f32[64,128]{1,0:T(8,128)}) fusion(f32[128,128]{1,0:T(8,128)S(1)} %shard_map.77), kind=kLoop, calls=%fused_computation | loop fusion | bytes 131072 | tf_op jit(solution)/shard_map/slice | solution.py:541

commit v4 on v3

--- a/solution.py
+++ b/solution.py
@@ -20,7 +20,7 @@
 B = 128
 FB = 16
 JITTER = 0.25
-KERN_EARLY = 7
+KERN_EARLY = 6
 SPREAD = math.sqrt(4.0 * math.log2(math.e))
 SINE = [(-1) ** k * (2.0 * math.pi) ** (2 * k + 1) / math.factorial(2 * k + 1) for k in range(6)]
 
@@ -93,7 +93,7 @@
     out_ref,
     pts, tgt, noise, omega, phase, weights,
     prm_own, bundle, ptw, ptsj, ptsi, pside, prior_s, halves, rhs_s, low, low_z, right, kern, outb, rcv,
-    mom_z, mom_p, cur_z, cur_p, send, recv, local,
+    mom_z, mom_p, cur_z, cur_p, mixes, send, recv, local,
 ):
     nx, nz, ny = sizes
     np_, half = nx * ny, nz // 2
@@ -154,9 +154,9 @@
     near_z = sorted(range(1, nz), key=lambda d: hops(d, nz))
     far_z = near_z[::-1]
 
-    def plane_dev(d):
+    def plane_dev(d, core=c):
         dx, dy = dxy(d)
-        return (xs[dx], z, ys[dy], c)
+        return (xs[dx], z, ys[dy], core)
 
     def plane_slot(d):
         dx, dy = dxy(d)
@@ -176,9 +176,9 @@
 
         for d in far_p:
             greet(plane_dev(d))
+            greet(plane_dev(d, oc))
         for d in far_z:
             greet(zdev(d, c))
-            greet(zdev(d, oc))
         greet(twin)
 
         turn = 1.0 / (2.0 * math.pi)
@@ -201,7 +201,7 @@
         twice = jnp.where((wide == deep) | (wide == deep + S), 1.0, 0.0).astype(BF16)
         prm_own[0] = (packed + mm(w1, once)).astype(BF16)
         prm_own[1] = mm(w2, twice).astype(BF16)
-        pl.semaphore_wait(bar, 1 + 2 * (nz - 1) + np_ - 1)
+        pl.semaphore_wait(bar, 1 + (nz - 1) + 2 * (np_ - 1))
 
     mine = lax.rem(z, 2) == c
     zslot = lax.div(z, 2)
@@ -260,7 +260,6 @@
         pside[0] = jnp.concatenate([none, b1, b1, b1, ones, none[:32]], 0).astype(BF16)
         pside[1] = jnp.concatenate([none, b2, b2, none[:48]], 0).astype(BF16)
         pside[2] = jnp.concatenate([none, b3, none[:56]], 0).astype(BF16)
-        prior_s[...] = jnp.zeros_like(prior_s)
         for t in range(half):
             two = jnp.concatenate([ptsi[2 * t], ptsi[2 * t + 1]], 1)
             right[t] = exponent_right(two).astype(BF16)
@@ -282,39 +281,50 @@
         spans = sorted(range(nx), key=lambda d: hops(d, nx))
         for stage in range(2):
             columns = []
-            for dx in spans:
-                base = xs[(nx - dx) % nx] * ny
-                group = bundle.at[stage, pl.ds(0, ny - 1)] if dx == 0 else bundle.at[stage, pl.ds(base, ny)]
-                got("prm%d" % stage, dx, group)
-                columns.append(base)
-            for bases in (columns[:2], columns[2:]):
+
+            def columns_in(some):
+                for dx in some:
+                    base = xs[(nx - dx) % nx] * ny
+                    group = bundle.at[stage, pl.ds(0, ny - 1)] if dx == 0 else bundle.at[stage, pl.ds(base, ny)]
+                    got("prm%d" % stage, dx, group)
+                    columns.append(base)
+
+            columns_in(spans)
+
+            def features(bases, lanes):
                 pick = [(base + q, k) for k in range(2) for base in bases for q in range(ny)]
                 part = jnp.concatenate([bundle[stage, slot, k] for slot, k in pick], 0)
                 rest = jnp.concatenate([bundle[stage, base + q, 2] for base in bases for q in range(ny)], 0)
                 cut = rest.shape[0]
-                turns = mm(part, pside[0]) + mm(part, pside[1]) + mm(part, pside[2])
+                turns = mm(part, pside[0, :, lanes]) + mm(part, pside[1, :, lanes]) + mm(part, pside[2, :, lanes])
                 feats = cos_turns(turns)
                 f1 = feats.astype(BF16)
                 f2 = (feats - f1.astype(F32)).astype(BF16)
                 total = (mm(part, f1, flip) + mm(part, f2, flip))[:S]
-                prior_s[...] += total + mm(rest, f1[:cut], flip)[:S] + mm(rest, f1[cut:], flip)[S:]
+                return total + mm(rest, f1[:cut], flip)[:S] + mm(rest, f1[cut:], flip)[S:]
+
+            couples = (columns[:2], columns[2:])
+            if stage == 0:
+                prior_s[...] = sum(features(bases, slice(0, 2 * B)) for bases in couples)
+            else:
+                rcv[2, 1] = prior_s[:, B:] + sum(features(bases, slice(B, 2 * B)) for bases in couples)
+                put("prior", 0, rcv.at[2, 1], rcv.at[2, 0], twin)
+                sent("prior", rcv.at[2, 1])
+                prior_own = prior_s[:, :B] + sum(features(bases, slice(0, B)) for bases in couples)
 
     with jax.named_scope("f_swap"):
-        rcv[2, 1] = prior_s[:, B:]
-        put("prior", 0, rcv.at[2, 1], rcv.at[2, 0], twin)
-        sent("prior", rcv.at[2, 1])
         for copy in arrivals[4:]:
             copy.wait()
         got("prior", 0, rcv.at[2, 0])
         scale = math.sqrt(2.0 / nfeat)
-        prior = scale * (prior_s[:, :B] + rcv[2, 0])
+        prior = scale * (prior_own + rcv[2, 0])
         rhs = tgt[...] - prior - 0.5 * noise[...]
         rhs_s[0] = prior
         rhs_s[1] = rhs
         low[0, c * np_ + p] = rhs.astype(BF16)
         low_z[0, z] = rhs.astype(BF16)
 
-    def matvec(n, first, each, last):
+    def matvec(n, first, blend, each, last):
         pn, dn, zn, on = "low%d_p" % n, "low%d_d" % n, "low%d_z" % n, "out%d" % n
         own = low.at[n, c * np_ + p]
         with jax.named_scope("g%d_send" % n):
@@ -357,30 +367,25 @@
 
         spans = sorted(range(nx), key=lambda d: hops(d, nx))
         with jax.named_scope("i%d_gather_a" % n):
-            own_group(spans[0])
-            own_group(spans[1])
+            for dx in spans:
+                own_group(dx)
         with jax.named_scope("i%d_gather_b" % n):
-            add_tiles([(c, spans[0]), (c, spans[1])], True)
-        with jax.named_scope("i%d_gather_c" % n):
-            own_group(spans[2])
-            own_group(spans[3])
-            twin_group(spans[0])
-        with jax.named_scope("i%d_gather_d" % n):
-            add_tiles([(c, spans[2]), (c, spans[3]), (oc, spans[0])], False)
+            add_tiles([(c, dx) for dx in spans], True)
+            flush()
         with jax.named_scope("i%d_gather_e" % n):
             got(zn, 0, low_z.at[n, pl.ds(0, nz - 1)])
-            twin_group(spans[1])
-            twin_group(spans[2])
-            twin_group(spans[3])
-            flush()
+            for dx in spans:
+                twin_group(dx)
 
         with jax.named_scope("j%d_tiles" % n):
             sums = None
             for t in range(half):
-                out = times(oc, spans[1], t) + times(oc, spans[2], t) + times(oc, spans[3], t)
+                out = times(oc, spans[0], t)
+                for dx in spans[1:]:
+                    out = out + times(oc, dx, t)
                 for s in range(2):
                     zz = 2 * t + s
-                    piece = outb[n, zz] + out[:, s * B:(s + 1) * B]
+                    piece = blend(zz, outb[n, zz] + out[:, s * B:(s + 1) * B])
                     outb[n, zz] = piece
                     terms = each(zz, piece)
                     sums = terms if sums is None else [a + b for a, b in zip(sums, terms)]
@@ -397,27 +402,27 @@
         return total
 
     def z_start(name, buf, value):
-        zc = 2 * z + c
-        buf[zc] = value
+        buf[z] = value
         for d in far_z:
-            put(name + "_z", 0, buf.at[zc], buf.at[zc], zdev(d, c))
-            put(name + "_z", 0, buf.at[zc], buf.at[zc], zdev(d, oc))
-        put(name + "_z", 0, buf.at[zc], buf.at[zc], twin)
-        sent(name + "_z", buf.at[pl.ds(0, 2 * nz - 1)])
+            put(name + "_z", 0, buf.at[z], buf.at[z], zdev(d, c))
+        sent(name + "_z", buf.at[pl.ds(0, nz - 1)])
 
     def z_end(name, buf):
-        got(name + "_z", 0, buf.at[pl.ds(0, 2 * nz - 1)])
-        return sum_all(buf, 2 * nz)
+        got(name + "_z", 0, buf.at[pl.ds(0, nz - 1)])
+        return sum_all(buf, nz)
 
     def p_start(name, buf, value):
-        buf[p] = value
+        slot = c * np_ + p
+        buf[slot] = value
         for d in far_p:
-            put(name + "_p", 0, buf.at[p], buf.at[p], plane_dev(d))
-        sent(name + "_p", buf.at[pl.ds(0, np_ - 1)])
+            put(name + "_p", 0, buf.at[slot], buf.at[slot], plane_dev(d, oc))
+            put(name + "_p", 0, buf.at[slot], buf.at[slot], plane_dev(d))
+        put(name + "_p", 0, buf.at[slot], buf.at[slot], twin)
+        sent(name + "_p", buf.at[pl.ds(0, 2 * np_ - 1)])
 
     def p_end(name, buf):
-        got(name + "_p", 0, buf.at[pl.ds(0, np_ - 1)])
-        return sum_all(buf, np_)
+        got(name + "_p", 0, buf.at[pl.ds(0, 2 * np_ - 1)])
+        return sum_all(buf, 2 * np_)
 
     def sum_all(buf, count):
         parts = [buf[k] for k in range(count)]
@@ -437,40 +442,59 @@
     def each0(zz, piece):
         return [piece * low_z[0, zz].astype(F32)]
 
+    def blend0(zz, piece):
+        return piece
+
+    def near_alpha(row):
+        both = spread(row)
+        dot, norm = jnp.maximum(both[:S], 0.0), both[S:]
+        return jnp.where(norm > 0.0, norm, 1.0) / jnp.where(norm > 0.0, dot + JITTER * norm, 1.0)
+
     def last0(sums):
         r = rhs_s[1]
         p_start("cur0", cur_p.at[0], lane_sums([*sums, r * r]))
-        z_start("cur0", cur_z.at[0], p_end("cur0", cur_p.at[0]))
-
-    k0 = matvec(0, first0, each0, last0)
+        row = p_end("cur0", cur_p.at[0])
+        z_start("cur0", cur_z.at[0], row)
+        rhs_s[4] = near_alpha(row)
+
+    k0 = matvec(0, first0, blend0, each0, last0)
     with jax.named_scope("m_alpha"):
         rhs = rhs_s[1]
         q1 = k0 + JITTER * rhs
         rhs_s[2] = k0
+        basis = rhs - rhs_s[4] * q1
+        low[1, c * np_ + p] = basis.astype(BF16)
+        low_z[1, z] = basis.astype(BF16)
+        rhs_s[3] = q1
+
+    def first1():
+        r, k, q1 = rhs_s[1], rhs_s[2], rhs_s[3]
         sums = spread(z_end("cur0", cur_z.at[0]))
         m0 = sums[S:]
         alpha = m0 / (sums[:S] + JITTER * m0)
-        r1 = rhs - alpha * q1
-        low[1, c * np_ + p] = r1.astype(BF16)
-        low_z[1, z] = r1.astype(BF16)
-        rhs_s[3] = r1
+        new = r - alpha * q1
+        rhs_s[3] = new
         rhs_s[4] = alpha
         rhs_s[5] = m0
-
-    def first1():
-        r, k, new = rhs_s[1], rhs_s[2], rhs_s[3]
         sums = lane_sums([new * new, new * r, new * k, r * k])
         z_start("mom", mom_z, jnp.concatenate([sums[:, :128], sums[:, 128:]], 0))
+        for zz in range(nz):
+            mixes[zz] = alpha / near_alpha(cur_z[0, zz])
+
+    def blend1(zz, piece):
+        mix = mixes[z]
+        return mix * piece + (1.0 - mix) * outb[0, zz]
 
     def each1(zz, piece):
-        return [piece * low_z[1, zz].astype(F32), piece * low_z[0, zz].astype(F32)]
+        mix, r = mixes[zz], low_z[0, zz].astype(F32)
+        return [piece * (mix * low_z[1, zz].astype(F32) + (1.0 - mix) * r), piece * r]
 
     def last1(sums):
         p_start("cur1", cur_p.at[1], lane_sums(sums))
         p_start("mom", mom_p, z_end("mom", mom_z))
         z_start("cur1", cur_z.at[1], p_end("cur1", cur_p.at[1]))
 
-    k1 = matvec(1, first1, each1, last1)
+    k1 = matvec(1, first1, blend1, each1, last1)
     with jax.named_scope("n_finish"):
         prior, r, k0, r1, alpha, m0 = (rhs_s[k] for k in range(6))
         mom = p_end("mom", mom_p)
@@ -527,10 +551,11 @@
             pltpu.VMEM((half, 2 * np_ * B, 2 * B), BF16),
             pltpu.VMEM((2, nz, S, B), F32),
             pltpu.VMEM((3, nz, S, B), F32),
-            pltpu.VMEM((2 * nz, 2, 128), F32),
-            pltpu.VMEM((np_, 2, 128), F32),
-            pltpu.VMEM((2, 2 * nz, 1, 128), F32),
-            pltpu.VMEM((2, np_, 1, 128), F32),
+            pltpu.VMEM((nz, 2, 128), F32),
+            pltpu.VMEM((2 * np_, 2, 128), F32),
+            pltpu.VMEM((2, nz, 1, 128), F32),
+            pltpu.VMEM((2, 2 * np_, 1, 128), F32),
+            pltpu.VMEM((nz, S, B), F32),
             pltpu.SemaphoreType.DMA((len(SENDS()),)),
             pltpu.SemaphoreType.DMA((sum(count for _, count in RECVS(nx)),)),
             pltpu.SemaphoreType.DMA((6,)),

time: 59.5 us -> 58.3 us (0.980)
  Pallas kernels: 58.1 us -> 56.9 us
    pallas_call x1, Pallas kernels: 58.1 us -> 56.9 us  [body(): pl.pallas_call(functools.partial(kernel, sizes), out_shape=block, in_spec...]
where the time goes in v4:
time: 58.3 us; the launch traced here: 58.2 us
  Pallas kernels  56.9 us (98%)
  between operations  0.64 us (1%)
  local copies, waits for them, and re-layouts  0.63 us (1%)
    pallas_call x1, Pallas kernels, body(): pl.pallas_call(functools.partial(kernel, sizes), out_shape=block, in_spec...  56.9 us

profile of v4, /device:TPU:1, one launch (start us, length us, event | category | flops | bytes accessed | tf_op | source)
XLA Modules:
  0.0 58.2 jit_solution(16236950448466438026)
XLA Ops:
  0.6 56.9 %shard_map.77 = f32[128,128]{1,0:T(8,128)S(1)} custom-call(f32[8,128]{1,0:T(8,128)} %pts_hbm.1, f32[1,128]{1,0:T(1,128)} %bitcast.2, f32[64,128]{1,0:T(8,128)} %noise_hbm.1, f32[8,16]{1,0:T(8,128)} %omega_hbm.1, f32[1,16]{1,0:T(1,128)} %bitcast.3, f32[16,64]{1,0:T(8,128)} %weights_hbm.1), custom_call_target="tpu_custom_call" | custom-call | tf_op jit(solution)/shard_map/pallas_call | solution.py:527
  57.6 0.6 %fusion = (f32[64,128]{1,0:T(8,128)}, f32[64,128]{1,0:T(8,128)}) fusion(f32[128,128]{1,0:T(8,128)S(1)} %shard_map.77), kind=kLoop, calls=%fused_computation | loop fusion | bytes 131072 | tf_op jit(solution)/shard_map/slice | solution.py:566

commit v5 on v4

--- a/solution.py
+++ b/solution.py
@@ -20,7 +20,7 @@
 B = 128
 FB = 16
 JITTER = 0.25
-KERN_EARLY = 6
+KERN_EARLY = 8
 SPREAD = math.sqrt(4.0 * math.log2(math.e))
 SINE = [(-1) ** k * (2.0 * math.pi) ** (2 * k + 1) / math.factorial(2 * k + 1) for k in range(6)]
 
@@ -367,21 +367,26 @@
 
         spans = sorted(range(nx), key=lambda d: hops(d, nx))
         with jax.named_scope("i%d_gather_a" % n):
-            for dx in spans:
+            own_group(spans[0])
+        with jax.named_scope("i%d_gather_b" % n):
+            add_tiles([(c, spans[0])], True)
+        with jax.named_scope("i%d_gather_c" % n):
+            for dx in spans[1:]:
                 own_group(dx)
-        with jax.named_scope("i%d_gather_b" % n):
-            add_tiles([(c, dx) for dx in spans], True)
+            twin_group(spans[0])
+        with jax.named_scope("i%d_gather_d" % n):
+            add_tiles([(c, dx) for dx in spans[1:]] + [(oc, spans[0])], False)
             flush()
         with jax.named_scope("i%d_gather_e" % n):
             got(zn, 0, low_z.at[n, pl.ds(0, nz - 1)])
-            for dx in spans:
+            for dx in spans[1:]:
                 twin_group(dx)
 
         with jax.named_scope("j%d_tiles" % n):
             sums = None
             for t in range(half):
-                out = times(oc, spans[0], t)
-                for dx in spans[1:]:
+                out = times(oc, spans[1], t)
+                for dx in spans[2:]:
                     out = out + times(oc, dx, t)
                 for s in range(2):
                     zz = 2 * t + s

time: 58.3 us -> 57.9 us (level)
  no operation moved by 1% of the time
where the time goes in v5:
time: 57.9 us; the launch traced here: 57.8 us
  Pallas kernels  56.5 us (98%)
  between operations  0.64 us (1%)
  local copies, waits for them, and re-layouts  0.63 us (1%)
    pallas_call x1, Pallas kernels, body(): pl.pallas_call(functools.partial(kernel, sizes), out_shape=block, in_spec...  56.5 us

profile of v5, /device:TPU:1, one launch (start us, length us, event | category | flops | bytes accessed | tf_op | source)
XLA Modules:
  0.0 57.8 jit_solution(12894010363025337029)
XLA Ops:
  0.6 56.5 %shard_map.77 = f32[128,128]{1,0:T(8,128)S(1)} custom-call(f32[8,128]{1,0:T(8,128)} %pts_hbm.1, f32[1,128]{1,0:T(1,128)} %bitcast.2, f32[64,128]{1,0:T(8,128)} %noise_hbm.1, f32[8,16]{1,0:T(8,128)} %omega_hbm.1, f32[1,16]{1,0:T(1,128)} %bitcast.3, f32[16,64]{1,0:T(8,128)} %weights_hbm.1), custom_call_target="tpu_custom_call" | custom-call | tf_op jit(solution)/shard_map/pallas_call | solution.py:532
  57.1 0.6 %fusion = (f32[64,128]{1,0:T(8,128)}, f32[64,128]{1,0:T(8,128)}) fusion(f32[128,128]{1,0:T(8,128)S(1)} %shard_map.77), kind=kLoop, calls=%fused_computation | loop fusion | bytes 131072 | tf_op jit(solution)/shard_map/slice | solution.py:571

commit v6 on v5

--- a/solution.py
+++ b/solution.py
@@ -34,7 +34,7 @@
 
 def RECVS(nx):
     several = {"prm_z": 4}
-    for name in ("prm0", "prm1", "low0_p", "low0_d", "low1_p", "low1_d"):
+    for name in ("low0_p", "low0_d", "low1_p", "low1_d"):
         several[name] = nx
     return [(name, several.get(name, 1)) for name in SENDS()]
 
@@ -243,7 +243,7 @@
             bundle[stage, p, 2] = jnp.where(left_lanes, one[1].astype(F32), two[1].astype(F32)).astype(BF16)
             name = "prm%d" % stage
             for d in far_p:
-                put(name, d // ny, bundle.at[stage, p], bundle.at[stage, p], plane_dev(d))
+                put(name, 0, bundle.at[stage, p], bundle.at[stage, p], plane_dev(d))
             sent(name, bundle.at[stage, pl.ds(0, np_ - 1)])
 
     with jax.named_scope("c_points"):
@@ -285,10 +285,9 @@
             def columns_in(some):
                 for dx in some:
                     base = xs[(nx - dx) % nx] * ny
-                    group = bundle.at[stage, pl.ds(0, ny - 1)] if dx == 0 else bundle.at[stage, pl.ds(base, ny)]
-                    got("prm%d" % stage, dx, group)
                     columns.append(base)
 
+            got("prm%d" % stage, 0, bundle.at[stage, pl.ds(0, np_ - 1)])
             columns_in(spans)
 
             def features(bases, lanes):

time: 57.9 us -> 57.8 us (level)
  no operation moved by 1% of the time
where the time goes in v6:
time: 57.8 us; the launch traced here: 57.7 us
  Pallas kernels  56.4 us (98%)
  between operations  0.64 us (1%)
  local copies, waits for them, and re-layouts  0.63 us (1%)
    pallas_call x1, Pallas kernels, body(): pl.pallas_call(functools.partial(kernel, sizes), out_shape=block, in_spec...  56.4 us

profile of v6, /device:TPU:1, one launch (start us, length us, event | category | flops | bytes accessed | tf_op | source)
XLA Modules:
  0.0 57.7 jit_solution(7328682887480646850)
XLA Ops:
  0.6 56.4 %shard_map.77 = f32[128,128]{1,0:T(8,128)S(1)} custom-call(f32[8,128]{1,0:T(8,128)} %pts_hbm.1, f32[1,128]{1,0:T(1,128)} %bitcast.2, f32[64,128]{1,0:T(8,128)} %noise_hbm.1, f32[8,16]{1,0:T(8,128)} %omega_hbm.1, f32[1,16]{1,0:T(1,128)} %bitcast.3, f32[16,64]{1,0:T(8,128)} %weights_hbm.1), custom_call_target="tpu_custom_call" | custom-call | tf_op jit(solution)/shard_map/pallas_call | solution.py:531
  57.1 0.6 %fusion = (f32[64,128]{1,0:T(8,128)}, f32[64,128]{1,0:T(8,128)}) fusion(f32[128,128]{1,0:T(8,128)S(1)} %shard_map.77), kind=kLoop, calls=%fused_computation | loop fusion | bytes 131072 | tf_op jit(solution)/shard_map/slice | solution.py:570
